TPU v7x, 32 devices: a whole 2x2x4 slice. The times are simulated.
32 devices in a mesh: dp: 8 (over y, x, core), tp: 4 (over z).
Axes of the slice: x: 2, y: 2, z: 4, core: 2. Of those that a mesh axis runs over, the one named last changes fastest.
Arguments:
- tokens: bfloat16 [32768, 768], P('dp'), may hold values from -6 to 6
- cotangent: bfloat16 [32768, 768], P('dp'), may hold values from -6 to 6
- size_tags: int32 [8], P('dp'), may hold values from 0 to 1
- time_index: int32 [32], replicated, may hold values from 0 to 999
- class_index: int32 [32], replicated, may hold values from 0 to 999
- time_table: bfloat16 [1000, 768], replicated, may hold values from -6 to 6
- class_table: bfloat16 [1000, 768], replicated, may hold values from -6 to 6
- w_mod: bfloat16 [768, 4608], P(None, 'tp'), may hold values from -0.21875 to 0.21875
- w_qkv: bfloat16 [768, 2304], P(None, 'tp'), may hold values from -0.21875 to 0.21875
- conv_qkv: bfloat16 [9, 2304], P(None, 'tp'), may hold values from -2 to 2
- w_out: bfloat16 [768, 768], P('tp'), may hold values from -0.75 to 0.75
- w_up: bfloat16 [768, 3072], P(None, 'tp'), may hold values from -0.21875 to 0.21875
- conv_ffn: bfloat16 [9, 3072], P(None, 'tp'), may hold values from -2 to 2
- w_down: bfloat16 [3072, 768], P('tp'), may hold values from -0.109375 to 0.109375
Outputs:
- mixed: bfloat16 [32768, 768], P('dp')
- grad_tokens: float32 [32768, 768], P(('dp', 'tp'))
- grad_time: float32 [1000, 768], P(None, 'dp')
- grad_class: float32 [1000, 768], P(None, 'dp')
- grad_mod: float32 [768, 4608], P('dp', 'tp')
- grad_qkv: float32 [768, 2304], P('dp', 'tp')
- grad_conv_qkv: float32 [9, 2304], P(None, ('tp', 'dp'))
- grad_out: float32 [768, 768], P('tp', 'dp')
- grad_up: float32 [768, 3072], P('dp', 'tp')
- grad_conv_ffn: float32 [9, 3072], P(None, ('tp', 'dp'))
- grad_down: float32 [3072, 768], P('tp', 'dp')
Inputs may be any that keep to these rules, and one draw needn't show every extreme that they name: `size_tags`: 1: the buffer holds one item of 64 x 64 tokens and only its slot 0 is used; 0: four items, one in each quadrant of the grid, in slots of quadrant order.
All inputs are finite; a program needn't handle non-finite values.
Results may differ from a plain program's by a relative error of at most 0.018.
The roundings to bfloat16 on the way count: a program that leaves them out, or rounds other values in their place, can miss the bound.
Values may be sent and summed in bfloat16 or wider, within the bound.
A program may use at most 384 MiB of HBM per device.

v0:
```python
from functools import partial
import jax
import jax.numpy as jnp
from jax import lax
from jax.sharding import PartitionSpec as P

D = 768
HEAD_SIZE = 64
SIDE = 64
SLOTS = 4


def layer_norm(values):
    average = jnp.mean(values, axis=-1, keepdims=True)
    centred = values - average
    variance = jnp.mean(centred * centred, axis=-1, keepdims=True)
    return centred * lax.rsqrt(variance + 1e-06)


def item_ids(size_tag, grid_side):
    row_index = lax.broadcasted_iota(jnp.int32, (grid_side, grid_side), 0)
    col_index = lax.broadcasted_iota(jnp.int32, (grid_side, grid_side), 1)
    quadrant = row_index // (grid_side // 2) * 2 + col_index // (grid_side // 2)
    return jnp.where(size_tag == 1, jnp.zeros_like(quadrant), quadrant)


def depthwise(field, kernel, labels):
    grid_side = field.shape[0]
    padded = jnp.pad(field, ((1, 1), (1, 1), (0, 0)))
    padded_ids = jnp.pad(labels, 1, constant_values=-1)
    result = jnp.zeros_like(field)
    for tap_index in range(9):
        row_off = tap_index // 3
        col_off = tap_index % 3
        moved = padded[row_off : row_off + grid_side, col_off : col_off + grid_side]
        same_item = (
            padded_ids[row_off : row_off + grid_side, col_off : col_off + grid_side] == labels
        )
        result = result + kernel[tap_index] * jnp.where(
            same_item[:, :, None], moved, jnp.zeros_like(moved)
        )
    return result


def unshuffle(field):
    half_side = field.shape[0] // 2
    trailing = field.shape[2:]
    shaped = field.reshape((half_side, 2, half_side, 2) + trailing)
    order = (1, 3, 0, 2) + tuple(range(4, 4 + len(trailing)))
    return shaped.transpose(order).reshape((4, half_side * half_side) + trailing)


def shuffle(groups, grid_side):
    half_side = grid_side // 2
    trailing = groups.shape[2:]
    shaped = groups.reshape((2, 2, half_side, half_side) + trailing)
    order = (2, 0, 3, 1) + tuple(range(4, 4 + len(trailing)))
    return shaped.transpose(order).reshape((grid_side, grid_side) + trailing)


def attend(input_query, input_keys, input_values, allowed):
    scale_factor = HEAD_SIZE ** (-0.5)
    logit_scores = (
        jnp.einsum("yoe,goe->oyg", input_query, input_keys, preferred_element_type=jnp.float32)
        * scale_factor
    )
    logit_scores = jnp.where(allowed[None], logit_scores, -jnp.inf)
    row_top = jnp.max(logit_scores, axis=-1, keepdims=True)
    expo = jnp.exp(logit_scores - row_top)
    totals = jnp.sum(expo, axis=-1, keepdims=True)
    probabilities = (expo / totals).astype(jnp.bfloat16)
    result = jnp.einsum(
        "xbg,gxy->bxy", probabilities, input_values, preferred_element_type=jnp.float32
    ).astype(jnp.bfloat16)
    log_sums = (row_top + jnp.log(totals))[:, :, 0].T
    return (result, log_sums)


def attend_back(input_query, input_keys, input_values, allowed, gradient_result, log_sums):
    scale_factor = HEAD_SIZE ** (-0.5)
    logit_scores = (
        jnp.einsum("yoe,goe->oyg", input_query, input_keys, preferred_element_type=jnp.float32)
        * scale_factor
    )
    logit_scores = jnp.where(allowed[None], logit_scores, -jnp.inf)
    probabilities = jnp.exp(logit_scores - log_sums.T[:, :, None])
    grad_probs = jnp.einsum(
        "yoe,goe->oyg", gradient_result, input_values, preferred_element_type=jnp.float32
    )
    row_dots = jnp.sum(grad_probs * probabilities, axis=-1, keepdims=True)
    gradient_scores = (probabilities * (grad_probs - row_dots)).astype(jnp.bfloat16)
    grad_query = (
        jnp.einsum("xbg,gxy->bxy", gradient_scores, input_keys, preferred_element_type=jnp.float32)
        * scale_factor
    )
    grad_keys = (
        jnp.einsum("zew,ezb->wzb", gradient_scores, input_query, preferred_element_type=jnp.float32)
        * scale_factor
    )
    grad_values = jnp.einsum(
        "zew,ezb->wzb",
        probabilities.astype(jnp.bfloat16),
        gradient_result,
        preferred_element_type=jnp.float32,
    )
    return jnp.stack([grad_query, grad_keys, grad_values], axis=2)


def group_forward(block, allowed, size_tag):
    input_query = block[:, :, 0]
    input_keys = block[:, :, 1]
    input_values = block[:, :, 2]
    return attend(input_query, input_keys, input_values, allowed)


def group_backward(operands, allowed, size_tag):
    block, grad_block, log_sums = operands
    input_query = block[:, :, 0]
    input_keys = block[:, :, 1]
    input_values = block[:, :, 2]
    return attend_back(input_query, input_keys, input_values, allowed, grad_block, log_sums)


def modulate(values, shift_part, scale_part):
    return layer_norm(values) * (1.0 + scale_part) + shift_part


def per_device(
    tokens,
    cotangent,
    size_tags,
    time_index,
    class_index,
    time_table,
    class_table,
    w_mod,
    w_qkv,
    conv_qkv,
    w_out,
    w_up,
    conv_ffn,
    w_down,
):
    tp_count = lax.axis_size("tp")
    tp_rank = lax.axis_index("tp")
    dp_rank = lax.axis_index("dp")
    size_tag = size_tags[0]
    tok_count = tokens.shape[0]
    half_side = SIDE // 2
    heads_dev = w_out.shape[0] // HEAD_SIZE
    qkv_width = w_qkv.shape[1]
    hidden_width = w_up.shape[1]
    my_times = lax.dynamic_slice_in_dim(time_index, dp_rank * SLOTS, SLOTS)
    my_labels = lax.dynamic_slice_in_dim(class_index, dp_rank * SLOTS, SLOTS)
    condition = jnp.take(time_table, my_times, axis=0).astype(jnp.float32) + jnp.take(
        class_table, my_labels, axis=0
    ).astype(jnp.float32)
    activated = jax.nn.silu(condition).astype(jnp.bfloat16)
    mod_part = jnp.dot(activated, w_mod, preferred_element_type=jnp.float32)
    modulation = lax.all_gather(mod_part, "tp", axis=1, tiled=True)
    per_quad = jnp.where(
        size_tag == 1, jnp.broadcast_to(modulation[0:1], modulation.shape), modulation
    )
    quad_grid = per_quad.reshape(2, 1, 2, 1, 6 * D)
    shift_one = quad_grid[..., 0:D]
    scale_one = quad_grid[..., D : 2 * D]
    gate_one = quad_grid[..., 2 * D : 3 * D]
    shift_two = quad_grid[..., 3 * D : 4 * D]
    scale_two = quad_grid[..., 4 * D : 5 * D]
    gate_two = quad_grid[..., 5 * D : 6 * D]
    labels_grid = item_ids(size_tag, SIDE)
    group_labels = item_ids(size_tag, half_side).reshape(-1)
    allowed = group_labels[:, None] == group_labels[None, :]
    grid = tokens.astype(jnp.float32).reshape(2, half_side, 2, half_side, D)
    hidden_one = modulate(grid, shift_one, scale_one).astype(jnp.bfloat16).reshape(tok_count, D)
    projected = jnp.dot(hidden_one, w_qkv, preferred_element_type=jnp.float32)

    def conv_queries(values, kernel):
        return depthwise(values.reshape(SIDE, SIDE, qkv_width), kernel, labels_grid)

    mixed_float, conv_pull = jax.vjp(conv_queries, projected, conv_qkv.astype(jnp.float32))
    mixed_qkv = mixed_float.astype(jnp.bfloat16)
    grouped = unshuffle(mixed_qkv.reshape(SIDE, SIDE, heads_dev, 3, HEAD_SIZE))
    attended, log_sums = lax.map(
        partial(group_forward, allowed=allowed, size_tag=size_tag), grouped
    )
    heads_out = shuffle(attended, SIDE).reshape(tok_count, heads_dev * HEAD_SIZE)
    attention = lax.psum(
        jnp.dot(heads_out, w_out, preferred_element_type=jnp.float32).astype(jnp.bfloat16), "tp"
    ).astype(jnp.float32)
    after_attention = grid + gate_one * attention.reshape(grid.shape)
    hidden_two = (
        modulate(after_attention, shift_two, scale_two).astype(jnp.bfloat16).reshape(tok_count, D)
    )
    upward = jnp.dot(hidden_two, w_up, preferred_element_type=jnp.float32)

    def activate(values, kernel):
        convolved = depthwise(values.reshape(SIDE, SIDE, hidden_width), kernel, labels_grid)
        return jax.nn.gelu(convolved, approximate=False).reshape(tok_count, hidden_width)

    act_float, act_pull = jax.vjp(activate, upward, conv_ffn.astype(jnp.float32))
    activation = act_float.astype(jnp.bfloat16)
    feed = lax.psum(
        jnp.dot(activation, w_down, preferred_element_type=jnp.float32).astype(jnp.bfloat16), "tp"
    ).astype(jnp.float32)
    result = after_attention + gate_two * feed.reshape(grid.shape)
    mixed = result.reshape(tok_count, D).astype(jnp.bfloat16)
    gradient_result = cotangent.astype(jnp.float32).reshape(grid.shape)
    grad_feed = (gate_two * gradient_result).astype(jnp.bfloat16).reshape(tok_count, D)
    grad_activation = jnp.dot(grad_feed, w_down.T, preferred_element_type=jnp.float32)
    grad_down_w = jnp.einsum("tf,td->fd", activation, grad_feed, preferred_element_type=jnp.float32)
    grad_upward, grad_kernel_ffn = act_pull(grad_activation)
    grad_up_low = grad_upward.astype(jnp.bfloat16)
    grad_up_w = jnp.einsum("td,tf->df", hidden_two, grad_up_low, preferred_element_type=jnp.float32)
    grad_hidden_two = lax.psum_scatter(
        jnp.dot(grad_up_low, w_up.T, preferred_element_type=jnp.float32).astype(jnp.bfloat16),
        "tp",
        scatter_dimension=0,
        tiled=True,
    ).astype(jnp.float32)
    quarter_rows = SIDE // tp_count
    quarter_tokens = tok_count // tp_count
    quarter_start = tp_rank * quarter_tokens
    quad_row = tp_rank * quarter_rows // half_side
    quarter_shape = (quarter_rows, 2, half_side, D)
    mods_quarter = lax.dynamic_index_in_dim(
        per_quad.reshape(2, 2, 6 * D), quad_row, 0, keepdims=False
    ).reshape(1, 2, 1, 6 * D)
    flat_after = after_attention.reshape(tok_count, D)
    after_quarter = lax.dynamic_slice_in_dim(flat_after, quarter_start, quarter_tokens, 0).reshape(
        quarter_shape
    )
    modulated_two, ln_pull_two = jax.vjp(
        modulate, after_quarter, mods_quarter[..., 3 * D : 4 * D], mods_quarter[..., 4 * D : 5 * D]
    )
    grad_after_ln, grad_shift_two, grad_scale_two = ln_pull_two(
        grad_hidden_two.reshape(quarter_shape)
    )
    grad_ln_rows = lax.all_gather(
        grad_after_ln.reshape(quarter_tokens, D).astype(jnp.bfloat16), "tp", axis=0, tiled=True
    ).astype(jnp.float32)
    flat_grad_result = gradient_result.reshape(tok_count, D)
    grad_after = flat_grad_result + grad_ln_rows
    feed_quarter = lax.dynamic_slice_in_dim(feed, quarter_start, quarter_tokens, 0).reshape(
        quarter_shape
    )
    result_grad_quarter = lax.dynamic_slice_in_dim(
        flat_grad_result, quarter_start, quarter_tokens, 0
    ).reshape(quarter_shape)
    grad_gate_two = jnp.sum(result_grad_quarter * feed_quarter, axis=(0, 2))
    grad_attention = (
        (gate_one * grad_after.reshape(grid.shape)).astype(jnp.bfloat16).reshape(tok_count, D)
    )
    grad_heads = jnp.dot(grad_attention, w_out.T, preferred_element_type=jnp.float32).astype(
        jnp.bfloat16
    )
    grad_out_w = jnp.einsum(
        "tc,td->cd", heads_out, grad_attention, preferred_element_type=jnp.float32
    )
    after_grad_quarter = lax.dynamic_slice_in_dim(grad_after, quarter_start, quarter_tokens, 0)
    attention_quarter = lax.dynamic_slice_in_dim(attention, quarter_start, quarter_tokens, 0)
    grad_gate_one = jnp.sum(
        (after_grad_quarter * attention_quarter).reshape(quarter_shape), axis=(0, 2)
    )
    grad_grouped = unshuffle(grad_heads.reshape(SIDE, SIDE, heads_dev, HEAD_SIZE))
    grad_qkv_groups = lax.map(
        partial(group_backward, allowed=allowed, size_tag=size_tag),
        (grouped, grad_grouped, log_sums),
    )
    grad_mixed = shuffle(grad_qkv_groups, SIDE).reshape(SIDE, SIDE, qkv_width)
    grad_projected, grad_kernel_qkv = conv_pull(grad_mixed)
    grad_proj_low = grad_projected.astype(jnp.bfloat16)
    grad_qkv_w = jnp.einsum(
        "td,tc->dc", hidden_one, grad_proj_low, preferred_element_type=jnp.float32
    )
    grad_hidden_one = lax.psum_scatter(
        jnp.dot(grad_proj_low, w_qkv.T, preferred_element_type=jnp.float32).astype(jnp.bfloat16),
        "tp",
        scatter_dimension=0,
        tiled=True,
    ).astype(jnp.float32)
    tokens_quarter = lax.dynamic_slice_in_dim(
        grid.reshape(tok_count, D), quarter_start, quarter_tokens, 0
    ).reshape(quarter_shape)
    modulated_one, ln_pull_one = jax.vjp(
        modulate, tokens_quarter, mods_quarter[..., 0:D], mods_quarter[..., D : 2 * D]
    )
    grad_tokens_ln, grad_shift_one, grad_scale_one = ln_pull_one(
        grad_hidden_one.reshape(quarter_shape)
    )
    grad_tokens = after_grad_quarter + grad_tokens_ln.reshape(quarter_tokens, D)
    quad_rows = jnp.concatenate(
        [
            grad_shift_one.reshape(2, D),
            grad_scale_one.reshape(2, D),
            grad_gate_one,
            grad_shift_two.reshape(2, D),
            grad_scale_two.reshape(2, D),
            grad_gate_two,
        ],
        axis=-1,
    )
    row_pick = (lax.iota(jnp.int32, 2) == quad_row)[:, None, None]
    grad_quads = jnp.where(row_pick, quad_rows[None], jnp.zeros_like(quad_rows[None])).reshape(
        4, 6 * D
    )
    merged_slot = jnp.concatenate(
        [jnp.sum(grad_quads, axis=0, keepdims=True), jnp.zeros((SLOTS - 1, 6 * D), jnp.float32)],
        axis=0,
    )
    grad_slots = jnp.where(size_tag == 1, merged_slot, grad_quads)
    grad_mod_cols = lax.psum_scatter(
        grad_slots.astype(jnp.bfloat16), "tp", scatter_dimension=1, tiled=True
    ).astype(jnp.float32)
    grad_mod_w = jnp.dot(
        activated.astype(jnp.float32).T, grad_mod_cols, precision=lax.Precision.HIGHEST
    )
    grad_activated = jnp.dot(
        grad_mod_cols, w_mod.astype(jnp.float32).T, precision=lax.Precision.HIGHEST
    )
    silu_value, silu_pull = jax.vjp(jax.nn.silu, condition)
    grad_cond_part = silu_pull(grad_activated)[0]
    grad_condition = lax.psum(grad_cond_part, "tp")
    grad_cols = lax.all_to_all(grad_condition, "dp", split_axis=1, concat_axis=0, tiled=True)
    time_iota = lax.broadcasted_iota(jnp.int32, (time_index.shape[0], time_table.shape[0]), 1)
    time_hits = (time_index[:, None] == time_iota).astype(jnp.float32)
    grad_time = jnp.dot(time_hits.T, grad_cols, precision=lax.Precision.HIGHEST)
    class_iota = lax.broadcasted_iota(jnp.int32, (class_index.shape[0], class_table.shape[0]), 1)
    class_hits = (class_index[:, None] == class_iota).astype(jnp.float32)
    grad_class = jnp.dot(class_hits.T, grad_cols, precision=lax.Precision.HIGHEST)
    summed_qkv, summed_conv_qkv, summed_out, summed_mod, summed_up, summed_conv_ffn, summed_down = (
        lax.psum_scatter(grad_qkv_w, "dp", scatter_dimension=0, tiled=True),
        lax.psum_scatter(grad_kernel_qkv, "dp", scatter_dimension=1, tiled=True),
        lax.psum_scatter(grad_out_w, "dp", scatter_dimension=1, tiled=True),
        lax.psum_scatter(grad_mod_w, "dp", scatter_dimension=0, tiled=True),
        lax.psum_scatter(grad_up_w, "dp", scatter_dimension=0, tiled=True),
        lax.psum_scatter(grad_kernel_ffn, "dp", scatter_dimension=1, tiled=True),
        lax.psum_scatter(grad_down_w, "dp", scatter_dimension=1, tiled=True),
    )
    return (
        mixed,
        grad_tokens,
        grad_time,
        grad_class,
        summed_mod,
        summed_qkv,
        summed_conv_qkv,
        summed_out,
        summed_up,
        summed_conv_ffn,
        summed_down,
    )


def solution(mesh):
    in_specs = (
        P("dp", None),
        P("dp", None),
        P("dp"),
        P(),
        P(),
        P(),
        P(),
        P(None, "tp"),
        P(None, "tp"),
        P(None, "tp"),
        P("tp", None),
        P(None, "tp"),
        P(None, "tp"),
        P("tp", None),
    )
    out_specs = (
        P("dp", None),
        P(("dp", "tp"), None),
        P(None, "dp"),
        P(None, "dp"),
        P("dp", "tp"),
        P("dp", "tp"),
        P(None, ("tp", "dp")),
        P("tp", "dp"),
        P("dp", "tp"),
        P(None, ("tp", "dp")),
        P("tp", "dp"),
    )
    return jax.shard_map(
        per_device, mesh=mesh, in_specs=in_specs, out_specs=out_specs, check_vma=False
    )
```

profile of v0, /device:TPU:0, one launch (start us, length us, event | category | flops | bytes accessed | tf_op | source)
XLA Modules:
  0.0 1967.9 jit_solution(16814510556548511663)
XLA Ops:
  22.4 15.0 all_gather.6
  45.4 7.7 fusion.67
  53.2 39.4 %add_convert_fusion = bf16[64,64,576]{2,1,0:T(8,128)(2,1)} fusion(f32[64,64,576]{2,1,0:T(8,128)} %fusion.67, f32[576]{0:T(1024)S(1)} %get-tuple-element.161, f32[576]{0:T(1024)S(1)} %copy-done.55, f32[576]{0:T(1024)S(1)} %copy-done.57, f32[576]{0:T(1024)S(1)} %copy-done.59, f32[576]{0:T(1024)S(1)} %copy-done.61, f32[576]{0:T(1024)S(1)} %copy-done.63, ...), kind=kLoop, calls=%fused_computation.168 | loop fusion | flops 61341696 | bytes 14209280 | tf_op jit(solution)/shard_map/convert_element_type | solution.py:182
  92.7 23.2 %reshape_reshape.12 = bf16[32,2,32,2,3,3,64]{6,5,4,3,2,1,0:T(4,128)(2,1)} reshape(bf16[64,64,576]{2,1,0:T(8,128)(2,1)} %add_convert_fusion) | data formatting | bytes 9437184 | tf_op jit(solution)/shard_map/reshape;reshape | solution.py:48
  115.8 10.7 copy.51
  126.5 9.8 copy.52
  136.3 91.1 %while.24 = (s32[]{:T(128)}, bf16[4,1024,3,64]{1,3,2,0:T(8,128)(2,1)S(1)}, f32[4,1024,3]{1,2,0:T(4,128)}, bf16[4,1024,3,3,64]{1,4,2,3,0:T(8,128)(2,1)}, s32[1024]{0:T(1024)S(1)}, /*index=5*/s32[]{:T(128)}) while((s32[]{:T(128)}, bf16[4,1024,3,64]{1,3,2,0:T(8,128)(2,1)S(1)}, f32[4,1024,3]{1,2,0:T(4,128)}, ...), condition=%wide.region_5.7_spmd.clone, body=%wide.region_2.6_spmd.clone.sunk | while | flops 844297216 | bytes 45989976 | solution.py:184
  144.4 7.3 fusion.146
  167.2 7.3 fusion.146
  236.8 8.9 reshape_reshape.13
  252.0 224.0 %all-reduce.44.cloned.1.call-done = bf16[4096,768]{1,0:T(8,128)(2,1)} async-done(((bf16[4096,768]{1,0:T(8,128)(2,1)}), bf16[4096,768]{1,0:T(8,128)(2,1)}) %all-reduce.44.cloned.1.call-update) | async-done | bytes 6291472 | tf_op jit(solution)/shard_map/psum | solution.py:188
  476.0 11.2 fusion.101
  500.6 8.2 fusion.65
  508.8 57.6 %multiply_convert_fusion.1 = (bf16[64,64,768]{2,1,0:T(8,128)(2,1)S(1)}, f32[64,64,768]{2,1,0:T(8,128)}, f32[64,64,768]{2,1,0:T(8,128)}) fusion(pred[64,64]{1,0:T(8,128)(4,1)S(1)} %copy-done.33, f32[768]{0:T(1024)S(1)} %get-tuple-element.152, pred[64,64]{1,0:T(8,128)(4,1)S(1)} %copy-done.15, f32[768]{0:T(1024)S(1)} %get-tuple-element.153, ...), kind=kLoop, calls=%fused_computation.118 | loop fusion | flops 283115520 | bytes 44100608 | tf_op jit(solution)/shard_map/convert_element_type | solution.py:202
  576.1 221.8 %all-reduce.46.cloned.1.call-done = bf16[4096,768]{1,0:T(8,128)(2,1)} async-done(((bf16[4096,768]{1,0:T(8,128)(2,1)}), bf16[4096,768]{1,0:T(8,128)(2,1)}) %all-reduce.46.cloned.1.call-update) | async-done | bytes 6291472 | tf_op jit(solution)/shard_map/psum | solution.py:203
  798.0 14.7 fusion.46
  812.6 70.9 %multiply_reduce_fusion.9 = (f32[768]{0:T(1024)}, f32[768]{0:T(1024)}, f32[768]{0:T(1024)}, f32[768]{0:T(1024)}, f32[768]{0:T(1024)}, /*index=5*/f32[768]{0:T(10...) fusion(f32[64,64,768]{2,1,0:T(8,128)} %fusion.65, ...), kind=kOutput, calls=%fused_computation.107 | convolution fusion | flops 4960803840 | bytes 70449152 | tf_op jit(solution)/shard_map/dot_general | solution.py:210
  883.6 32.2 %multiply_select_fusion.8 = (f32[64,64,768]{2,1,0:T(8,128)S(1)}, f32[64,64,768]{2,1,0:T(8,128)}, f32[64,64,768]{2,1,0:T(8,128)}, f32[64,64,768]{2,1,0:T(8,128)},...) fusion(f32[64,64,768]{2,1,0:T(8,128)} %get-tuple-element.254, ...), kind=kLoop, calls=%fused_computation.116 | loop fusion | flops 47185920 | bytes 113299456 | tf_op jit(solution)/shard_map/transpose(jvp(jit(_where)))/select_n | solution.py:39
  915.7 19.0 pad_add_fusion
  934.8 29.6 %fusion.47 = bf16[64,64,768]{2,1,0:T(8,128)(2,1)} fusion(f32[64,64,768]{2,1,0:T(8,128)} %get-tuple-element.210, f32[64,64,768]{2,1,0:T(8,128)} %get-tuple-element.216, f32[64,64,768]{2,1,0:T(8,128)} %get-tuple-element.217, f32[64,64,768]{2,1,0:T(8,128)} %get-tuple-element.218, f32[64,64,768]{2,1,0:T(8,128)} %get-tuple-element.219, f32[66,66,768]{2,1,0:T(8,128)} %pad_add_fusion), kind=kLoop, calls=%fused_computation.88 | loop fusion | flops 18874368 | bytes 81788928 | tf_op jit(solution)/shard_map/convert.1
  964.4 10.0 convolution_convert_fusion.2
  979.0 105.3 %reduce-scatter.17.cloned.1.call-done = bf16[1024,768]{1,0:T(8,128)(2,1)} async-done(((bf16[4096,768]{1,0:T(8,128)(2,1)}), bf16[1024,768]{1,0:T(8,128)(2,1)}) %reduce-scatter.17.cloned.1.call-update) | async-done | bytes 1572880 | tf_op jit(solution)/shard_map/reduce_scatter | solution.py:215
  1092.3 115.9 %all-gather.2.cloned.1.call-done = bf16[4096,768]{1,0:T(8,128)(2,1)} async-done(((bf16[1024,768]{1,0:T(8,128)(2,1)}), bf16[4096,768]{1,0:T(8,128)(2,1)}) %all-gather.2.cloned.1.call-update) | async-done | bytes 6291472 | tf_op jit(solution)/shard_map/all_gather | solution.py:239
  1208.2 10.9 fusion.43
  1229.0 8.5 reshape_reshape.14
  1246.3 109.3 %while.25 = (s32[]{:T(128)}, f32[4,1024,3,3,64]{1,4,2,3,0:T(8,128)}, bf16[4,1024,3,3,64]{1,4,2,3,0:T(8,128)(2,1)}, f32[4,1024,3]{1,2,0:T(4,128)}, bf16[4,1024,3,...) while((s32[]{:T(128)}, f32[4,1024,3,3,64]{1,4,2,3,0:T(8,128)}, ...), condition=%wide.region_17.19_spmd.clone, body=%wide.region_15.18_spmd.clone.sunk | while | flops 2063070208 | bytes 117145728 | solution.py:266
  1355.6 13.8 copy.59
  1369.4 26.1 %copy.60 = f32[32,2,32,2,3,3,64]{6,5,4,3,2,1,0:T(4,128)} copy(f32[32,2,32,2,3,3,64]{6,2,0,5,4,3,1:T(8,128)} %bitcast.260) | data formatting | bytes 18874368 | tf_op jit(solution)/shard_map/transpose | solution.py:58
  1395.5 26.3 %reshape_reshape.15 = f32[64,64,576]{2,1,0:T(8,128)} reshape(f32[32,2,32,2,3,3,64]{6,5,4,3,2,1,0:T(4,128)} %copy.60) | data formatting | bytes 18874368 | tf_op jit(solution)/shard_map/reshape;reshape | solution.py:270
  1422.0 43.9 %multiply_reduce_fusion.20 = (f32[576]{0:T(1024)S(1)}, f32[576]{0:T(1024)S(1)}, f32[576]{0:T(1024)S(1)}, f32[576]{0:T(1024)S(1)}, f32[576]{0:T(1024)S(1)}, /*ind...) fusion(f32[64,64,576]{2,1,0:T(8,128)} %reshape_reshape.15, ...), kind=kLoop, calls=%fused_computation.159 | loop fusion | flops 66055104 | bytes 28367360 | tf_op jit(solution)/shard_map/transpose(jvp())/reduce_sum | solution.py:39
  1465.9 29.3 %multiply_select_fusion.16 = (f32[64,64,576]{2,1,0:T(8,128)}, f32[64,64,576]{2,1,0:T(8,128)}, f32[64,64,576]{2,1,0:T(8,128)}, f32[64,64,576]{2,1,0:T(8,128)}, f3...) fusion(f32[64,64,576]{2,1,0:T(8,128)} %reshape_reshape.15, ...), kind=kLoop, calls=%fused_computation.167 | loop fusion | flops 35389440 | bytes 84981760 | tf_op jit(solution)/shard_map/transpose(jvp(jit(_where)))/select_n | solution.py:39
  1495.3 14.7 pad_add_fusion.6
  1509.9 20.1 %fusion.63 = bf16[64,64,576]{2,1,0:T(8,128)(2,1)} fusion(f32[64,64,576]{2,1,0:T(8,128)} %get-tuple-element.223, f32[64,64,576]{2,1,0:T(8,128)} %get-tuple-element.225, f32[64,64,576]{2,1,0:T(8,128)} %get-tuple-element.226, f32[64,64,576]{2,1,0:T(8,128)} %get-tuple-element.227, f32[64,64,576]{2,1,0:T(8,128)} %get-tuple-element.228, ...), kind=kLoop, calls=%fused_computation.146 | loop fusion | flops 14155776 | bytes 61341696 | tf_op jit(solution)/shard_map/convert
  1530.1 9.3 convolution_convert_fusion
  1539.7 8.7 convert_element_type.133
  1548.4 8.3 convert_element_type.117
  1561.0 8.3 convert_element_type.125
  1582.5 66.1 %reduce-scatter.19.cloned.1.call-done = bf16[1024,768]{1,0:T(8,128)(2,1)} async-done(((bf16[4096,768]{1,0:T(8,128)(2,1)}), bf16[1024,768]{1,0:T(8,128)(2,1)}) %reduce-scatter.19.cloned.1.call-update) | async-done | bytes 1572880 | tf_op jit(solution)/shard_map/reduce_scatter | solution.py:276
  1676.2 10.1 fusion.105
  1686.4 10.1 fusion.104
  1696.6 9.7 fusion.103
  1711.3 22.8 %reduce-scatter.33.cloned.1.call-done = f32[96,9]{1,0:T(8,128)} async-done(((f32[768,9]{1,0:T(8,128)}), f32[96,9]{1,0:T(8,128)}) %reduce-scatter.33.cloned.1.call-update) | async-done | bytes 3472
  1735.6 22.9 %all-reduce.40 = f32[9,576]{1,0:T(8,128)S(1)} all-reduce(f32[9,576]{1,0:T(8,128)S(1)} %pad_add_fusion.13), channel_id=7, replica_groups=mesh['dp'=8,'tp'=4] {'dp'}, use_global_device_ids=true, to_apply=%region_43.45.clone | all-reduce | flops 5184 | bytes 41472
  1760.2 19.3 psum.23
  1789.8 28.6 %reduce-scatter.27.cloned.1.call-done = f32[768,96]{0,1:T(8,128)} async-done(((f32[768,768]{0,1:T(8,128)}), f32[768,96]{0,1:T(8,128)}) %reduce-scatter.27.cloned.1.call-update) | async-done | bytes 294928 | tf_op jit(solution)/shard_map/reduce_scatter | solution.py:338
  1818.4 46.1 %reduce-scatter.25.cloned.1.call-done = f32[96,768]{1,0:T(8,128)} async-done(((f32[768,768]{1,0:T(8,128)}), f32[96,768]{1,0:T(8,128)}) %reduce-scatter.25.cloned.1.call-update) | async-done | bytes 294928 | tf_op jit(solution)/shard_map/reduce_scatter | solution.py:336
  1864.6 44.2 %reduce-scatter.23.cloned.1.call-done = f32[96,576]{1,0:T(8,128)} async-done(((f32[768,576]{1,0:T(8,128)}), f32[96,576]{1,0:T(8,128)}) %reduce-scatter.23.cloned.1.call-update) | async-done | bytes 221200 | tf_op jit(solution)/shard_map/reduce_scatter | solution.py:332
  1908.8 51.9 %reduce-scatter.21.cloned.1.call-done = f32[96,1152]{1,0:T(8,128)} async-done(((f32[768,1152]{1,0:T(8,128)}), f32[96,1152]{1,0:T(8,128)}) %reduce-scatter.21.cloned.1.call-update) | async-done | bytes 442384 | tf_op jit(solution)/shard_map/reduce_scatter | solution.py:335
  (404 shorter events, 339.6 us)
Async XLA Ops:
  7.2 468.7 %all-reduce.44.cloned.1.call-start = ((), (), s32[]{:S(2)}) async-start(), calls=%async_computation.10 | async-start | bytes 12582912 | tf_op jit(solution)/shard_map/psum | solution.py:188
  8.8 28.6 %copy-start.75 = (pred[4]{0:T(512)(128)(4,1)}, pred[4]{0:T(512)(128)(4,1)S(1)}, u32[]{:S(2)}) copy-start(pred[4]{0:T(512)(128)(4,1)S(1)} %get-tuple-element.202) | copy-start | bytes 16
  8.8 28.6 %copy-start.77 = (pred[4]{0:T(512)(128)(4,1)}, pred[4]{0:T(512)(128)(4,1)S(1)}, u32[]{:S(2)}) copy-start(pred[4]{0:T(512)(128)(4,1)S(1)} %get-tuple-element.255) | copy-start | bytes 16
  17.0 36.1 %copy-start.14 = (pred[64,64]{1,0:T(8,128)(4,1)}, pred[64,64]{1,0:T(8,128)(4,1)S(1)}, u32[]{:S(2)}) copy-start(pred[64,64]{1,0:T(8,128)(4,1)S(1)} %get-tuple-element.241) | copy-start | bytes 12292
  17.0 36.1 %copy-start.17 = (pred[64,64]{1,0:T(8,128)(4,1)}, pred[64,64]{1,0:T(8,128)(4,1)S(1)}, u32[]{:S(2)}) copy-start(pred[64,64]{1,0:T(8,128)(4,1)S(1)} %get-tuple-element.242) | copy-start | bytes 12292
  17.0 36.1 %copy-start.20 = (pred[64,64]{1,0:T(8,128)(4,1)}, pred[64,64]{1,0:T(8,128)(4,1)S(1)}, u32[]{:S(2)}) copy-start(pred[64,64]{1,0:T(8,128)(4,1)S(1)} %get-tuple-element.243) | copy-start | bytes 12292
  17.0 36.1 %copy-start.23 = (pred[64,64]{1,0:T(8,128)(4,1)}, pred[64,64]{1,0:T(8,128)(4,1)S(1)}, u32[]{:S(2)}) copy-start(pred[64,64]{1,0:T(8,128)(4,1)S(1)} %get-tuple-element.244) | copy-start | bytes 12292
  17.0 36.1 %copy-start.26 = (pred[64,64]{1,0:T(8,128)(4,1)}, pred[64,64]{1,0:T(8,128)(4,1)S(1)}, u32[]{:S(2)}) copy-start(pred[64,64]{1,0:T(8,128)(4,1)S(1)} %get-tuple-element.245) | copy-start | bytes 12292
  17.0 36.1 %copy-start.29 = (pred[64,64]{1,0:T(8,128)(4,1)}, pred[64,64]{1,0:T(8,128)(4,1)S(1)}, u32[]{:S(2)}) copy-start(pred[64,64]{1,0:T(8,128)(4,1)S(1)} %get-tuple-element.246) | copy-start | bytes 12292
  17.0 36.1 %copy-start.32 = (pred[64,64]{1,0:T(8,128)(4,1)}, pred[64,64]{1,0:T(8,128)(4,1)S(1)}, u32[]{:S(2)}) copy-start(pred[64,64]{1,0:T(8,128)(4,1)S(1)} %get-tuple-element.247) | copy-start | bytes 12292
  17.7 35.5 %copy-start.53 = (f32[576]{0:T(1024)}, f32[576]{0:T(1024)S(1)}, u32[]{:S(2)}) copy-start(f32[576]{0:T(1024)S(1)} %get-tuple-element.161) | copy-start | bytes 6916
  245.7 230.3 %copy-start.41 = (f32[2,2,768]{2,1,0:T(2,128)S(1)}, f32[2,2,768]{2,1,0:T(2,128)}, u32[]{:S(2)}) copy-start(f32[2,2,768]{2,1,0:T(2,128)} %get-tuple-element.237) | copy-start | bytes 36868
  251.8 546.1 %all-reduce.46.cloned.1.call-start = ((), (), s32[]{:S(2)}) async-start(), calls=%async_computation.11 | async-start | bytes 12582912 | tf_op jit(solution)/shard_map/psum | solution.py:203
  508.8 60.2 %copy-start.90 = (bf16[768,768]{1,0:T(8,128)(2,1)S(1)}, bf16[768,768]{1,0:T(8,128)(2,1)}, u32[]{:S(2)}) copy-start(bf16[768,768]{1,0:T(8,128)(2,1)} %param.33) | copy-start | bytes 3538948
  569.0 228.9 %copy-start.50 = (f32[2,2,768]{2,1,0:T(2,128)S(1)}, f32[2,2,768]{2,1,0:T(2,128)}, u32[]{:S(2)}) copy-start(f32[2,2,768]{2,1,0:T(2,128)} %get-tuple-element.234) | copy-start | bytes 36868
  576.1 508.2 %reduce-scatter.17.cloned.1.call-start = ((), (), s32[]{:S(2)}) async-start(), calls=%async_computation.12 | async-start | bytes 7864320 | tf_op jit(solution)/shard_map/reduce_scatter | solution.py:215
  934.8 29.6 %copy-start.92 = (bf16[768,768]{1,0:T(8,128)(2,1)S(1)}, bf16[768,768]{1,0:T(8,128)(2,1)}, u32[]{:S(2)}) copy-start(bf16[768,768]{1,0:T(8,128)(2,1)} %param.31) | copy-start | bytes 3538948
  974.4 233.7 %all-gather.2.cloned.1.call-start = ((), (), s32[]{:S(2)}) async-start(), calls=%async_computation.13 | async-start | bytes 7864320 | tf_op jit(solution)/shard_map/all_gather | solution.py:239
  979.0 229.2 %copy-start.42 = (f32[2,2,768]{2,1,0:T(2,128)S(1)}, f32[2,2,768]{2,1,0:T(2,128)}, u32[]{:S(2)}) copy-start(f32[2,2,768]{2,1,0:T(2,128)} %get-tuple-element.237) | copy-start | bytes 36868
  979.0 113.3 %copy-start.48 = (f32[1024]{0:T(1024)}, f32[1024]{0:T(1024)S(1)}, u32[]{:S(2)}) copy-start(f32[1024]{0:T(1024)S(1)} %broadcast_multiply_fusion.5) | copy-start | bytes 12292
  1092.2 556.4 %reduce-scatter.19.cloned.1.call-start = ((), (), s32[]{:S(2)}) async-start(), calls=%async_computation.14 | async-start | bytes 7864320 | tf_op jit(solution)/shard_map/reduce_scatter | solution.py:276
  1092.2 129.5 %copy-start.36 = (bf16[192,768]{1,0:T(8,128)(2,1)S(1)}, bf16[192,768]{1,0:T(8,128)(2,1)}, u32[]{:S(2)}) copy-start(bf16[192,768]{1,0:T(8,128)(2,1)} %param.30) | copy-start | bytes 884740
  1395.5 26.4 %copy-start.16 = (pred[64,64]{1,0:T(8,128)(4,1)S(1)}, pred[64,64]{1,0:T(8,128)(4,1)}, u32[]{:S(2)}) copy-start(pred[64,64]{1,0:T(8,128)(4,1)} %copy-done.14) | copy-start | bytes 12292
  1395.5 26.4 %copy-start.19 = (pred[64,64]{1,0:T(8,128)(4,1)S(1)}, pred[64,64]{1,0:T(8,128)(4,1)}, u32[]{:S(2)}) copy-start(pred[64,64]{1,0:T(8,128)(4,1)} %copy-done.17) | copy-start | bytes 12292
  1395.5 26.4 %copy-start.22 = (pred[64,64]{1,0:T(8,128)(4,1)S(1)}, pred[64,64]{1,0:T(8,128)(4,1)}, u32[]{:S(2)}) copy-start(pred[64,64]{1,0:T(8,128)(4,1)} %copy-done.20) | copy-start | bytes 12292
  1395.5 26.4 %copy-start.25 = (pred[64,64]{1,0:T(8,128)(4,1)S(1)}, pred[64,64]{1,0:T(8,128)(4,1)}, u32[]{:S(2)}) copy-start(pred[64,64]{1,0:T(8,128)(4,1)} %copy-done.23) | copy-start | bytes 12292
  1395.5 26.4 %copy-start.28 = (pred[64,64]{1,0:T(8,128)(4,1)S(1)}, pred[64,64]{1,0:T(8,128)(4,1)}, u32[]{:S(2)}) copy-start(pred[64,64]{1,0:T(8,128)(4,1)} %copy-done.26) | copy-start | bytes 12292
  1395.5 26.4 %copy-start.31 = (pred[64,64]{1,0:T(8,128)(4,1)S(1)}, pred[64,64]{1,0:T(8,128)(4,1)}, u32[]{:S(2)}) copy-start(pred[64,64]{1,0:T(8,128)(4,1)} %copy-done.29) | copy-start | bytes 12292
  1395.5 26.4 %copy-start.34 = (pred[64,64]{1,0:T(8,128)(4,1)S(1)}, pred[64,64]{1,0:T(8,128)(4,1)}, u32[]{:S(2)}) copy-start(pred[64,64]{1,0:T(8,128)(4,1)} %copy-done.32) | copy-start | bytes 12292
  1421.9 44.0 %copy-start.54 = (f32[576]{0:T(1024)S(1)}, f32[576]{0:T(1024)}, u32[]{:S(2)}) copy-start(f32[576]{0:T(1024)} %copy-done.53) | copy-start | bytes 6916
  1421.9 44.0 %copy-start.56 = (f32[576]{0:T(1024)S(1)}, f32[576]{0:T(1024)}, u32[]{:S(2)}) copy-start(f32[576]{0:T(1024)} %get-tuple-element.162) | copy-start | bytes 6916
  1421.9 44.0 %copy-start.58 = (f32[576]{0:T(1024)S(1)}, f32[576]{0:T(1024)}, u32[]{:S(2)}) copy-start(f32[576]{0:T(1024)} %get-tuple-element.163) | copy-start | bytes 6916
  1421.9 44.0 %copy-start.60 = (f32[576]{0:T(1024)S(1)}, f32[576]{0:T(1024)}, u32[]{:S(2)}) copy-start(f32[576]{0:T(1024)} %get-tuple-element.164) | copy-start | bytes 6916
  1421.9 44.0 %copy-start.62 = (f32[576]{0:T(1024)S(1)}, f32[576]{0:T(1024)}, u32[]{:S(2)}) copy-start(f32[576]{0:T(1024)} %get-tuple-element.165) | copy-start | bytes 6916
  1421.9 44.0 %copy-start.64 = (f32[576]{0:T(1024)S(1)}, f32[576]{0:T(1024)}, u32[]{:S(2)}) copy-start(f32[576]{0:T(1024)} %get-tuple-element.166) | copy-start | bytes 6916
  1422.0 44.0 %copy-start.66 = (f32[576]{0:T(1024)S(1)}, f32[576]{0:T(1024)}, u32[]{:S(2)}) copy-start(f32[576]{0:T(1024)} %get-tuple-element.167) | copy-start | bytes 6916
  1422.0 44.0 %copy-start.68 = (f32[576]{0:T(1024)S(1)}, f32[576]{0:T(1024)}, u32[]{:S(2)}) copy-start(f32[576]{0:T(1024)} %get-tuple-element.168) | copy-start | bytes 6916
  1539.4 167.0 %reduce-scatter.29.cloned.1.call-start = ((), (), s32[]{:S(2)}) async-start(), calls=%async_computation.19 | async-start | bytes 1474560
  1573.3 75.2 %copy-start.43 = (f32[2,768]{1,0:T(2,128)S(1)}, f32[2,768]{1,0:T(2,128)}, u32[]{:S(2)}) copy-start(f32[2,768]{1,0:T(2,128)} %get-tuple-element.238) | copy-start | bytes 18436
  1667.9 66.1 %reduce-scatter.33.cloned.1.call-start = ((), (), s32[]{:S(2)}) async-start(), calls=%async_computation.21 | async-start | bytes 442368
  1668.9 114.6 %reduce-scatter.31.cloned.1.call-start = ((), (), s32[]{:S(2)}) async-start(), calls=%async_computation.20 | async-start | bytes 884736
  1675.9 142.6 %reduce-scatter.27.cloned.1.call-start = ((), (), s32[]{:S(2)}) async-start(), calls=%async_computation.18 | async-start | bytes 2654208 | tf_op jit(solution)/shard_map/reduce_scatter | solution.py:338
  1686.3 178.3 %reduce-scatter.25.cloned.1.call-start = ((), (), s32[]{:S(2)}) async-start(), calls=%async_computation.17 | async-start | bytes 2654208 | tf_op jit(solution)/shard_map/reduce_scatter | solution.py:336
  1696.6 212.2 %reduce-scatter.23.cloned.1.call-start = ((), (), s32[]{:S(2)}) async-start(), calls=%async_computation.16 | async-start | bytes 2211840 | tf_op jit(solution)/shard_map/reduce_scatter | solution.py:332
  1706.3 81.2 %copy-start.88 = (s32[32]{0:T(128)S(1)}, s32[32]{0:T(128)}, u32[]{:S(2)}) copy-start(s32[32]{0:T(128)} %param.24) | copy-start | bytes 388
  1706.4 82.3 %copy-start.89 = (s32[32]{0:T(128)S(1)}, s32[32]{0:T(128)}, u32[]{:S(2)}) copy-start(s32[32]{0:T(128)} %param.23) | copy-start | bytes 388
  1706.4 254.3 %reduce-scatter.21.cloned.1.call-start = ((), (), s32[]{:S(2)}) async-start(), calls=%async_computation.15 | async-start | bytes 3981312 | tf_op jit(solution)/shard_map/reduce_scatter | solution.py:335
  1779.5 8.0 all-to-all-start
  (64 other events, 611.3 us)
Sparse Core Ops, SparseCore 0:
  251.9 223.9 all-reduce.43
  576.2 221.7 all-reduce.45
  974.5 109.6 reduce-scatter.16
  1092.3 115.8 all-gather.1
  1539.6 108.9 reduce-scatter.18
  1668.0 29.8 reduce-scatter.28
  1701.5 32.4 reduce-scatter.32
  1737.2 34.9 reduce-scatter.30
  1776.1 42.3 reduce-scatter.26
  1822.2 42.3 reduce-scatter.24
  1868.6 40.1 reduce-scatter.22
  1912.7 47.9 reduce-scatter.20
where the time goes:
time: 1980 us; the launch traced here: 1970 us
  waiting for transfers between devices  929 us (47%)
  other arithmetic  493 us (25%)
  matrix products  281 us (14%)
  local copies, waits for them, and re-layouts  184 us (9%)
  blocking collectives  57.2 us (3%)
    psum x1, waiting for transfers between devices, per_device(): lax.psum(jnp.dot(heads_out, w_out, preferred_element_type=jnp.float32).as...  224 us
    psum x1, waiting for transfers between devices, per_device(): lax.psum(jnp.dot(activation, w_down, preferred_element_type=jnp.float32)....  222 us
    all_gather x1, waiting for transfers between devices, per_device(): lax.all_gather(grad_after_ln.reshape(quarter_tokens, D).astype(jnp.bfloat...  116 us
    reduce_scatter x1, waiting for transfers between devices, per_device(): lax.psum_scatter(jnp.dot(grad_up_low, w_up.T, preferred_element_type=jnp....  105 us
    dot_general x1, matrix products, per_device(): jnp.dot(grad_feed, w_down.T, preferred_element_type=jnp.float32)  70.9 us
    reduce_scatter x1, waiting for transfers between devices, per_device(): lax.psum_scatter(jnp.dot(grad_proj_low, w_qkv.T, preferred_element_type=j...  66.1 us
    select_n x2, other arithmetic, depthwise(): jnp.where(same_item[:, :, None], moved, jnp.zeros_like(moved))  61.5 us
    convert_element_type x1, other arithmetic, per_device(): activation = act_float.astype(jnp.bfloat16)  57.6 us
  transfers between devices with their start and end apart: 13, of which 11 were waited for; matrix products, arithmetic and copies ran while one was open for 5% of the time, Pallas kernels for 0%

commit v1 on v0

--- a/solution.py
+++ b/solution.py
@@ -200,8 +200,12 @@
 
     act_float, act_pull = jax.vjp(activate, upward, conv_ffn.astype(jnp.float32))
     activation = act_float.astype(jnp.bfloat16)
-    feed = lax.psum(
-        jnp.dot(activation, w_down, preferred_element_type=jnp.float32).astype(jnp.bfloat16), "tp"
+    feed = jnp.sum(
+        lax.all_gather(
+            jnp.dot(activation, w_down, preferred_element_type=jnp.float32).astype(jnp.bfloat16),
+            "tp",
+        ),
+        axis=0,
     ).astype(jnp.float32)
     result = after_attention + gate_two * feed.reshape(grid.shape)
     mixed = result.reshape(tok_count, D).astype(jnp.bfloat16)

time: 1980 us -> 2200 us (1.11)
  waiting for transfers between devices: 929 us -> 1130 us
    all_gather x0 -> x1, waiting for transfers between devices: none -> 424 us  [per_device(): lax.all_gather(jnp.dot(activation, w_down, preferred_element_type=jnp.flo...]
    psum x1 -> x0, waiting for transfers between devices: 222 us -> none  [per_device(): lax.psum(jnp.dot(activation, w_down, preferred_element_type=jnp.float32)....]
  transfers between devices with their start and end apart: 13 -> 13, of which waited for: 11 -> 11; matrix products, arithmetic and copies ran while one was open for 5% -> 4% of each run, Pallas kernels for 0% -> 0%
where the time goes in v1:
time: 2200 us; the launch traced here: 2190 us
  waiting for transfers between devices  1130 us (51%)
  other arithmetic  509 us (23%)
  matrix products  283 us (13%)
  local copies, waits for them, and re-layouts  184 us (8%)
  blocking collectives  57.2 us (3%)
    all_gather x1, waiting for transfers between devices, per_device(): lax.all_gather(jnp.dot(activation, w_down, preferred_element_type=jnp.flo...  424 us
    psum x1, waiting for transfers between devices, per_device(): lax.psum(jnp.dot(heads_out, w_out, preferred_element_type=jnp.float32).as...  224 us
    all_gather x1, waiting for transfers between devices, per_device(): lax.all_gather(grad_after_ln.reshape(quarter_tokens, D).astype(jnp.bfloat...  116 us
    reduce_scatter x1, waiting for transfers between devices, per_device(): lax.psum_scatter(jnp.dot(grad_up_low, w_up.T, preferred_element_type=jnp....  105 us
    dot_general x1, matrix products, per_device(): jnp.dot(grad_feed, w_down.T, preferred_element_type=jnp.float32)  72.8 us
    reduce_scatter x1, waiting for transfers between devices, per_device(): lax.psum_scatter(jnp.dot(grad_proj_low, w_qkv.T, preferred_element_type=j...  66 us
    select_n x2, other arithmetic, depthwise(): jnp.where(same_item[:, :, None], moved, jnp.zeros_like(moved))  61.5 us
    convert_element_type x1, other arithmetic, per_device(): activation = act_float.astype(jnp.bfloat16)  57.2 us
  transfers between devices with their start and end apart: 13, of which 11 were waited for; matrix products, arithmetic and copies ran while one was open for 4% of the time, Pallas kernels for 0%

profile of v1, /device:TPU:0, one launch (start us, length us, event | category | flops | bytes accessed | tf_op | source)
XLA Modules:
  0.0 2186.4 jit_solution(6677423709995344879)
XLA Ops:
  22.4 15.0 all_gather.12
  45.4 7.7 fusion.67
  53.2 38.8 %add_convert_fusion = bf16[64,64,576]{2,1,0:T(8,128)(2,1)} fusion(f32[64,64,576]{2,1,0:T(8,128)} %fusion.67, f32[576]{0:T(1024)S(1)} %get-tuple-element.161, f32[576]{0:T(1024)S(1)} %copy-done.55, f32[576]{0:T(1024)S(1)} %copy-done.57, f32[576]{0:T(1024)S(1)} %copy-done.59, f32[576]{0:T(1024)S(1)} %copy-done.61, f32[576]{0:T(1024)S(1)} %copy-done.63, ...), kind=kLoop, calls=%fused_computation.168 | loop fusion | flops 61341696 | bytes 14209280 | tf_op jit(solution)/shard_map/convert_element_type | solution.py:182
  92.1 23.2 %reshape_reshape.12 = bf16[32,2,32,2,3,3,64]{6,5,4,3,2,1,0:T(4,128)(2,1)} reshape(bf16[64,64,576]{2,1,0:T(8,128)(2,1)} %add_convert_fusion) | data formatting | bytes 9437184 | tf_op jit(solution)/shard_map/reshape;reshape | solution.py:48
  115.2 10.7 copy.51
  125.9 9.7 copy.52
  135.6 91.4 %while.24 = (s32[]{:T(128)}, bf16[4,1024,3,64]{1,3,2,0:T(8,128)(2,1)S(1)}, f32[4,1024,3]{1,2,0:T(4,128)}, bf16[4,1024,3,3,64]{1,4,2,3,0:T(8,128)(2,1)}, s32[1024]{0:T(1024)S(1)}, /*index=5*/s32[]{:T(128)}) while((s32[]{:T(128)}, bf16[4,1024,3,64]{1,3,2,0:T(8,128)(2,1)S(1)}, f32[4,1024,3]{1,2,0:T(4,128)}, ...), condition=%wide.region_5.7_spmd.clone, body=%wide.region_2.6_spmd.clone.sunk | while | flops 844297216 | bytes 45989976 | solution.py:184
  144.0 7.3 fusion.146
  236.4 8.6 reshape_reshape.13
  251.3 224.0 %all-reduce.43.cloned.1.call-done = bf16[4096,768]{1,0:T(8,128)(2,1)} async-done(((bf16[4096,768]{1,0:T(8,128)(2,1)}), bf16[4096,768]{1,0:T(8,128)(2,1)}) %all-reduce.43.cloned.1.call-update) | async-done | bytes 6291472 | tf_op jit(solution)/shard_map/psum | solution.py:188
  475.3 11.2 fusion.101
  500.0 8.1 fusion.65
  508.1 57.2 %multiply_convert_fusion.1 = (bf16[64,64,768]{2,1,0:T(8,128)(2,1)S(1)}, f32[64,64,768]{2,1,0:T(8,128)}, f32[64,64,768]{2,1,0:T(8,128)}) fusion(pred[64,64]{1,0:T(8,128)(4,1)S(1)} %copy-done.33, f32[768]{0:T(1024)S(1)} %get-tuple-element.152, pred[64,64]{1,0:T(8,128)(4,1)S(1)} %copy-done.15, f32[768]{0:T(1024)S(1)} %get-tuple-element.153, ...), kind=kLoop, calls=%fused_computation.118 | loop fusion | flops 283115520 | bytes 44100608 | tf_op jit(solution)/shard_map/convert_element_type | solution.py:202
  574.9 424.2 %all-gather.6.cloned.1.call-done = bf16[16384,768]{1,0:T(8,128)(2,1)} async-done(((bf16[4096,768]{1,0:T(8,128)(2,1)}), bf16[16384,768]{1,0:T(8,128)(2,1)}) %all-gather.6.cloned.1.call-update) | async-done | bytes 25165840 | tf_op jit(solution)/shard_map/all_gather | solution.py:204
  999.1 17.5 reduce_sum.365
  1016.6 14.5 fusion.46
  1031.1 72.8 %multiply_reduce_fusion.9 = (f32[768]{0:T(1024)}, f32[768]{0:T(1024)}, f32[768]{0:T(1024)}, f32[768]{0:T(1024)}, f32[768]{0:T(1024)}, /*index=5*/f32[768]{0:T(10...) fusion(f32[64,64,768]{2,1,0:T(8,128)} %fusion.65, ...), kind=kOutput, calls=%fused_computation.107 | convolution fusion | flops 4960803840 | bytes 70449152 | tf_op jit(solution)/shard_map/dot_general | solution.py:214
  1103.9 32.2 %multiply_select_fusion.8 = (f32[64,64,768]{2,1,0:T(8,128)S(1)}, f32[64,64,768]{2,1,0:T(8,128)}, f32[64,64,768]{2,1,0:T(8,128)}, f32[64,64,768]{2,1,0:T(8,128)},...) fusion(f32[64,64,768]{2,1,0:T(8,128)} %get-tuple-element.254, ...), kind=kLoop, calls=%fused_computation.116 | loop fusion | flops 47185920 | bytes 113299456 | tf_op jit(solution)/shard_map/transpose(jvp(jit(_where)))/select_n | solution.py:39
  1136.1 19.0 pad_add_fusion
  1155.2 29.6 %fusion.47 = bf16[64,64,768]{2,1,0:T(8,128)(2,1)} fusion(f32[64,64,768]{2,1,0:T(8,128)} %get-tuple-element.210, f32[64,64,768]{2,1,0:T(8,128)} %get-tuple-element.216, f32[64,64,768]{2,1,0:T(8,128)} %get-tuple-element.217, f32[64,64,768]{2,1,0:T(8,128)} %get-tuple-element.218, f32[64,64,768]{2,1,0:T(8,128)} %get-tuple-element.219, f32[66,66,768]{2,1,0:T(8,128)} %pad_add_fusion), kind=kLoop, calls=%fused_computation.88 | loop fusion | flops 18874368 | bytes 81788928 | tf_op jit(solution)/shard_map/convert.2
  1184.8 10.1 convolution_convert_fusion.2
  1199.6 104.5 %reduce-scatter.17.cloned.1.call-done = bf16[1024,768]{1,0:T(8,128)(2,1)} async-done(((bf16[4096,768]{1,0:T(8,128)(2,1)}), bf16[1024,768]{1,0:T(8,128)(2,1)}) %reduce-scatter.17.cloned.1.call-update) | async-done | bytes 1572880 | tf_op jit(solution)/shard_map/reduce_scatter | solution.py:219
  1312.1 115.9 %all-gather.4.cloned.1.call-done = bf16[4096,768]{1,0:T(8,128)(2,1)} async-done(((bf16[1024,768]{1,0:T(8,128)(2,1)}), bf16[4096,768]{1,0:T(8,128)(2,1)}) %all-gather.4.cloned.1.call-update) | async-done | bytes 6291472 | tf_op jit(solution)/shard_map/all_gather | solution.py:243
  1428.0 10.9 fusion.43
  1448.7 8.5 reshape_reshape.14
  1466.0 109.1 %while.25 = (s32[]{:T(128)}, f32[4,1024,3,3,64]{1,4,2,3,0:T(8,128)}, bf16[4,1024,3,3,64]{1,4,2,3,0:T(8,128)(2,1)}, f32[4,1024,3]{1,2,0:T(4,128)}, bf16[4,1024,3,...) while((s32[]{:T(128)}, f32[4,1024,3,3,64]{1,4,2,3,0:T(8,128)}, ...), condition=%wide.region_17.19_spmd.clone, body=%wide.region_15.18_spmd.clone.sunk | while | flops 2063070208 | bytes 117145728 | solution.py:270
  1575.1 13.8 copy.59
  1588.9 26.1 %copy.60 = f32[32,2,32,2,3,3,64]{6,5,4,3,2,1,0:T(4,128)} copy(f32[32,2,32,2,3,3,64]{6,2,0,5,4,3,1:T(8,128)} %bitcast.261) | data formatting | bytes 18874368 | tf_op jit(solution)/shard_map/transpose | solution.py:58
  1615.1 26.3 %reshape_reshape.15 = f32[64,64,576]{2,1,0:T(8,128)} reshape(f32[32,2,32,2,3,3,64]{6,5,4,3,2,1,0:T(4,128)} %copy.60) | data formatting | bytes 18874368 | tf_op jit(solution)/shard_map/reshape;reshape | solution.py:274
  1641.5 42.9 %multiply_reduce_fusion.20 = (f32[576]{0:T(1024)S(1)}, f32[576]{0:T(1024)S(1)}, f32[576]{0:T(1024)S(1)}, f32[576]{0:T(1024)S(1)}, f32[576]{0:T(1024)S(1)}, /*ind...) fusion(f32[64,64,576]{2,1,0:T(8,128)} %reshape_reshape.15, ...), kind=kLoop, calls=%fused_computation.159 | loop fusion | flops 66055104 | bytes 28367360 | tf_op jit(solution)/shard_map/transpose(jvp())/reduce_sum | solution.py:39
  1684.5 29.3 %multiply_select_fusion.16 = (f32[64,64,576]{2,1,0:T(8,128)}, f32[64,64,576]{2,1,0:T(8,128)}, f32[64,64,576]{2,1,0:T(8,128)}, f32[64,64,576]{2,1,0:T(8,128)}, f3...) fusion(f32[64,64,576]{2,1,0:T(8,128)} %reshape_reshape.15, ...), kind=kLoop, calls=%fused_computation.167 | loop fusion | flops 35389440 | bytes 84981760 | tf_op jit(solution)/shard_map/transpose(jvp(jit(_where)))/select_n | solution.py:39
  1713.9 14.7 pad_add_fusion.6
  1728.6 20.2 fusion.63
  1748.8 9.4 convolution_convert_fusion
  1758.6 8.6 convert_element_type.137
  1767.2 8.3 convert_element_type.121
  1779.6 8.3 convert_element_type.129
  1801.3 66.0 %reduce-scatter.19.cloned.1.call-done = bf16[1024,768]{1,0:T(8,128)(2,1)} async-done(((bf16[4096,768]{1,0:T(8,128)(2,1)}), bf16[1024,768]{1,0:T(8,128)(2,1)}) %reduce-scatter.19.cloned.1.call-update) | async-done | bytes 1572880 | tf_op jit(solution)/shard_map/reduce_scatter | solution.py:280
  1894.8 10.1 fusion.105
  1905.0 10.1 fusion.104
  1915.3 9.8 fusion.103
  1929.9 22.8 %reduce-scatter.33.cloned.1.call-done = f32[96,9]{1,0:T(8,128)} async-done(((f32[768,9]{1,0:T(8,128)}), f32[96,9]{1,0:T(8,128)}) %reduce-scatter.33.cloned.1.call-update) | async-done | bytes 3472
  1954.4 22.9 %all-reduce.40 = f32[9,576]{1,0:T(8,128)S(1)} all-reduce(f32[9,576]{1,0:T(8,128)S(1)} %pad_add_fusion.13), channel_id=8, replica_groups=mesh['dp'=8,'tp'=4] {'dp'}, use_global_device_ids=true, to_apply=%region_43.45.clone | all-reduce | flops 5184 | bytes 41472
  1978.9 19.3 psum.15
  2008.5 28.7 %reduce-scatter.27.cloned.1.call-done = f32[768,96]{0,1:T(8,128)} async-done(((f32[768,768]{0,1:T(8,128)}), f32[768,96]{0,1:T(8,128)}) %reduce-scatter.27.cloned.1.call-update) | async-done | bytes 294928 | tf_op jit(solution)/shard_map/reduce_scatter | solution.py:342
  2037.2 46.1 %reduce-scatter.25.cloned.1.call-done = f32[96,768]{1,0:T(8,128)} async-done(((f32[768,768]{1,0:T(8,128)}), f32[96,768]{1,0:T(8,128)}) %reduce-scatter.25.cloned.1.call-update) | async-done | bytes 294928 | tf_op jit(solution)/shard_map/reduce_scatter | solution.py:340
  2083.3 44.2 %reduce-scatter.23.cloned.1.call-done = f32[96,576]{1,0:T(8,128)} async-done(((f32[768,576]{1,0:T(8,128)}), f32[96,576]{1,0:T(8,128)}) %reduce-scatter.23.cloned.1.call-update) | async-done | bytes 221200 | tf_op jit(solution)/shard_map/reduce_scatter | solution.py:336
  2127.5 51.9 %reduce-scatter.21.cloned.1.call-done = f32[96,1152]{1,0:T(8,128)} async-done(((f32[768,1152]{1,0:T(8,128)}), f32[96,1152]{1,0:T(8,128)}) %reduce-scatter.21.cloned.1.call-update) | async-done | bytes 442384 | tf_op jit(solution)/shard_map/reduce_scatter | solution.py:339
  (405 shorter events, 346.9 us)
Async XLA Ops:
  7.2 468.1 %all-reduce.43.cloned.1.call-start = ((), (), s32[]{:S(2)}) async-start(), calls=%async_computation.10 | async-start | bytes 12582912 | tf_op jit(solution)/shard_map/psum | solution.py:188
  8.8 28.6 %copy-start.75 = (pred[4]{0:T(512)(128)(4,1)}, pred[4]{0:T(512)(128)(4,1)S(1)}, u32[]{:S(2)}) copy-start(pred[4]{0:T(512)(128)(4,1)S(1)} %get-tuple-element.202) | copy-start | bytes 16
  8.8 28.6 %copy-start.77 = (pred[4]{0:T(512)(128)(4,1)}, pred[4]{0:T(512)(128)(4,1)S(1)}, u32[]{:S(2)}) copy-start(pred[4]{0:T(512)(128)(4,1)S(1)} %get-tuple-element.255) | copy-start | bytes 16
  17.0 36.1 %copy-start.14 = (pred[64,64]{1,0:T(8,128)(4,1)}, pred[64,64]{1,0:T(8,128)(4,1)S(1)}, u32[]{:S(2)}) copy-start(pred[64,64]{1,0:T(8,128)(4,1)S(1)} %get-tuple-element.241) | copy-start | bytes 12292
  17.0 36.1 %copy-start.17 = (pred[64,64]{1,0:T(8,128)(4,1)}, pred[64,64]{1,0:T(8,128)(4,1)S(1)}, u32[]{:S(2)}) copy-start(pred[64,64]{1,0:T(8,128)(4,1)S(1)} %get-tuple-element.242) | copy-start | bytes 12292
  17.0 36.1 %copy-start.20 = (pred[64,64]{1,0:T(8,128)(4,1)}, pred[64,64]{1,0:T(8,128)(4,1)S(1)}, u32[]{:S(2)}) copy-start(pred[64,64]{1,0:T(8,128)(4,1)S(1)} %get-tuple-element.243) | copy-start | bytes 12292
  17.0 36.1 %copy-start.23 = (pred[64,64]{1,0:T(8,128)(4,1)}, pred[64,64]{1,0:T(8,128)(4,1)S(1)}, u32[]{:S(2)}) copy-start(pred[64,64]{1,0:T(8,128)(4,1)S(1)} %get-tuple-element.244) | copy-start | bytes 12292
  17.0 36.1 %copy-start.26 = (pred[64,64]{1,0:T(8,128)(4,1)}, pred[64,64]{1,0:T(8,128)(4,1)S(1)}, u32[]{:S(2)}) copy-start(pred[64,64]{1,0:T(8,128)(4,1)S(1)} %get-tuple-element.245) | copy-start | bytes 12292
  17.0 36.1 %copy-start.29 = (pred[64,64]{1,0:T(8,128)(4,1)}, pred[64,64]{1,0:T(8,128)(4,1)S(1)}, u32[]{:S(2)}) copy-start(pred[64,64]{1,0:T(8,128)(4,1)S(1)} %get-tuple-element.246) | copy-start | bytes 12292
  17.0 36.1 %copy-start.32 = (pred[64,64]{1,0:T(8,128)(4,1)}, pred[64,64]{1,0:T(8,128)(4,1)S(1)}, u32[]{:S(2)}) copy-start(pred[64,64]{1,0:T(8,128)(4,1)S(1)} %get-tuple-element.247) | copy-start | bytes 12292
  17.7 35.5 %copy-start.53 = (f32[576]{0:T(1024)}, f32[576]{0:T(1024)S(1)}, u32[]{:S(2)}) copy-start(f32[576]{0:T(1024)S(1)} %get-tuple-element.161) | copy-start | bytes 6916
  245.0 230.3 %copy-start.41 = (f32[2,2,768]{2,1,0:T(2,128)S(1)}, f32[2,2,768]{2,1,0:T(2,128)}, u32[]{:S(2)}) copy-start(f32[2,2,768]{2,1,0:T(2,128)} %get-tuple-element.237) | copy-start | bytes 36868
  251.2 747.9 %all-gather.6.cloned.1.call-start = ((), (), s32[]{:S(2)}) async-start(), calls=%async_computation.18 | async-start | bytes 31457280 | tf_op jit(solution)/shard_map/all_gather | solution.py:204
  508.1 59.8 %copy-start.90 = (bf16[768,768]{1,0:T(8,128)(2,1)S(1)}, bf16[768,768]{1,0:T(8,128)(2,1)}, u32[]{:S(2)}) copy-start(bf16[768,768]{1,0:T(8,128)(2,1)} %param.33) | copy-start | bytes 3538948
  574.9 729.2 %reduce-scatter.17.cloned.1.call-start = ((), (), s32[]{:S(2)}) async-start(), calls=%async_computation.11 | async-start | bytes 7864320 | tf_op jit(solution)/shard_map/reduce_scatter | solution.py:219
  1155.2 29.6 %copy-start.92 = (bf16[768,768]{1,0:T(8,128)(2,1)S(1)}, bf16[768,768]{1,0:T(8,128)(2,1)}, u32[]{:S(2)}) copy-start(bf16[768,768]{1,0:T(8,128)(2,1)} %param.31) | copy-start | bytes 3538948
  1195.0 233.0 %all-gather.4.cloned.1.call-start = ((), (), s32[]{:S(2)}) async-start(), calls=%async_computation.12 | async-start | bytes 7864320 | tf_op jit(solution)/shard_map/all_gather | solution.py:243
  1199.6 228.4 %copy-start.42 = (f32[2,2,768]{2,1,0:T(2,128)S(1)}, f32[2,2,768]{2,1,0:T(2,128)}, u32[]{:S(2)}) copy-start(f32[2,2,768]{2,1,0:T(2,128)} %get-tuple-element.237) | copy-start | bytes 36868
  1199.6 112.5 %copy-start.48 = (f32[1024]{0:T(1024)}, f32[1024]{0:T(1024)S(1)}, u32[]{:S(2)}) copy-start(f32[1024]{0:T(1024)S(1)} %broadcast_multiply_fusion.5) | copy-start | bytes 12292
  1312.0 555.3 %reduce-scatter.19.cloned.1.call-start = ((), (), s32[]{:S(2)}) async-start(), calls=%async_computation.13 | async-start | bytes 7864320 | tf_op jit(solution)/shard_map/reduce_scatter | solution.py:280
  1312.1 129.5 %copy-start.36 = (bf16[192,768]{1,0:T(8,128)(2,1)S(1)}, bf16[192,768]{1,0:T(8,128)(2,1)}, u32[]{:S(2)}) copy-start(bf16[192,768]{1,0:T(8,128)(2,1)} %param.30) | copy-start | bytes 884740
  1615.0 26.4 %copy-start.16 = (pred[64,64]{1,0:T(8,128)(4,1)S(1)}, pred[64,64]{1,0:T(8,128)(4,1)}, u32[]{:S(2)}) copy-start(pred[64,64]{1,0:T(8,128)(4,1)} %copy-done.14) | copy-start | bytes 12292
  1615.0 26.4 %copy-start.19 = (pred[64,64]{1,0:T(8,128)(4,1)S(1)}, pred[64,64]{1,0:T(8,128)(4,1)}, u32[]{:S(2)}) copy-start(pred[64,64]{1,0:T(8,128)(4,1)} %copy-done.17) | copy-start | bytes 12292
  1615.0 26.4 %copy-start.22 = (pred[64,64]{1,0:T(8,128)(4,1)S(1)}, pred[64,64]{1,0:T(8,128)(4,1)}, u32[]{:S(2)}) copy-start(pred[64,64]{1,0:T(8,128)(4,1)} %copy-done.20) | copy-start | bytes 12292
  1615.0 26.4 %copy-start.25 = (pred[64,64]{1,0:T(8,128)(4,1)S(1)}, pred[64,64]{1,0:T(8,128)(4,1)}, u32[]{:S(2)}) copy-start(pred[64,64]{1,0:T(8,128)(4,1)} %copy-done.23) | copy-start | bytes 12292
  1615.0 26.4 %copy-start.28 = (pred[64,64]{1,0:T(8,128)(4,1)S(1)}, pred[64,64]{1,0:T(8,128)(4,1)}, u32[]{:S(2)}) copy-start(pred[64,64]{1,0:T(8,128)(4,1)} %copy-done.26) | copy-start | bytes 12292
  1615.1 26.4 %copy-start.31 = (pred[64,64]{1,0:T(8,128)(4,1)S(1)}, pred[64,64]{1,0:T(8,128)(4,1)}, u32[]{:S(2)}) copy-start(pred[64,64]{1,0:T(8,128)(4,1)} %copy-done.29) | copy-start | bytes 12292
  1615.1 26.4 %copy-start.34 = (pred[64,64]{1,0:T(8,128)(4,1)S(1)}, pred[64,64]{1,0:T(8,128)(4,1)}, u32[]{:S(2)}) copy-start(pred[64,64]{1,0:T(8,128)(4,1)} %copy-done.32) | copy-start | bytes 12292
  1615.1 26.4 %copy-start.40 = (pred[64,64]{1,0:T(8,128)(4,1)S(1)}, pred[64,64]{1,0:T(8,128)(4,1)}, u32[]{:S(2)}) copy-start(pred[64,64]{1,0:T(8,128)(4,1)} %get-tuple-element.240) | copy-start | bytes 12292
  1641.4 43.0 %copy-start.54 = (f32[576]{0:T(1024)S(1)}, f32[576]{0:T(1024)}, u32[]{:S(2)}) copy-start(f32[576]{0:T(1024)} %copy-done.53) | copy-start | bytes 6916
  1641.5 43.0 %copy-start.56 = (f32[576]{0:T(1024)S(1)}, f32[576]{0:T(1024)}, u32[]{:S(2)}) copy-start(f32[576]{0:T(1024)} %get-tuple-element.162) | copy-start | bytes 6916
  1641.5 43.0 %copy-start.58 = (f32[576]{0:T(1024)S(1)}, f32[576]{0:T(1024)}, u32[]{:S(2)}) copy-start(f32[576]{0:T(1024)} %get-tuple-element.163) | copy-start | bytes 6916
  1641.5 43.0 %copy-start.60 = (f32[576]{0:T(1024)S(1)}, f32[576]{0:T(1024)}, u32[]{:S(2)}) copy-start(f32[576]{0:T(1024)} %get-tuple-element.164) | copy-start | bytes 6916
  1641.5 43.0 %copy-start.62 = (f32[576]{0:T(1024)S(1)}, f32[576]{0:T(1024)}, u32[]{:S(2)}) copy-start(f32[576]{0:T(1024)} %get-tuple-element.165) | copy-start | bytes 6916
  1641.5 43.0 %copy-start.64 = (f32[576]{0:T(1024)S(1)}, f32[576]{0:T(1024)}, u32[]{:S(2)}) copy-start(f32[576]{0:T(1024)} %get-tuple-element.166) | copy-start | bytes 6916
  1641.5 43.0 %copy-start.66 = (f32[576]{0:T(1024)S(1)}, f32[576]{0:T(1024)}, u32[]{:S(2)}) copy-start(f32[576]{0:T(1024)} %get-tuple-element.167) | copy-start | bytes 6916
  1641.5 43.0 %copy-start.68 = (f32[576]{0:T(1024)S(1)}, f32[576]{0:T(1024)}, u32[]{:S(2)}) copy-start(f32[576]{0:T(1024)} %get-tuple-element.168) | copy-start | bytes 6916
  1758.2 166.9 %reduce-scatter.29.cloned.1.call-start = ((), (), s32[]{:S(2)}) async-start(), calls=%async_computation.19 | async-start | bytes 1474560
  1791.9 75.4 %copy-start.43 = (f32[2,768]{1,0:T(2,128)S(1)}, f32[2,768]{1,0:T(2,128)}, u32[]{:S(2)}) copy-start(f32[2,768]{1,0:T(2,128)} %get-tuple-element.238) | copy-start | bytes 18436
  1886.6 66.1 %reduce-scatter.33.cloned.1.call-start = ((), (), s32[]{:S(2)}) async-start(), calls=%async_computation.21 | async-start | bytes 442368
  1887.7 114.6 %reduce-scatter.31.cloned.1.call-start = ((), (), s32[]{:S(2)}) async-start(), calls=%async_computation.20 | async-start | bytes 884736
  1894.6 142.6 %reduce-scatter.27.cloned.1.call-start = ((), (), s32[]{:S(2)}) async-start(), calls=%async_computation.17 | async-start | bytes 2654208 | tf_op jit(solution)/shard_map/reduce_scatter | solution.py:342
  1904.9 178.4 %reduce-scatter.25.cloned.1.call-start = ((), (), s32[]{:S(2)}) async-start(), calls=%async_computation.16 | async-start | bytes 2654208 | tf_op jit(solution)/shard_map/reduce_scatter | solution.py:340
  1915.2 212.3 %reduce-scatter.23.cloned.1.call-start = ((), (), s32[]{:S(2)}) async-start(), calls=%async_computation.15 | async-start | bytes 2211840 | tf_op jit(solution)/shard_map/reduce_scatter | solution.py:336
  1925.0 81.3 %copy-start.88 = (s32[32]{0:T(128)S(1)}, s32[32]{0:T(128)}, u32[]{:S(2)}) copy-start(s32[32]{0:T(128)} %param.24) | copy-start | bytes 388
  1925.0 82.4 %copy-start.89 = (s32[32]{0:T(128)S(1)}, s32[32]{0:T(128)}, u32[]{:S(2)}) copy-start(s32[32]{0:T(128)} %param.23) | copy-start | bytes 388
  1925.0 254.4 %reduce-scatter.21.cloned.1.call-start = ((), (), s32[]{:S(2)}) async-start(), calls=%async_computation.14 | async-start | bytes 3981312 | tf_op jit(solution)/shard_map/reduce_scatter | solution.py:339
  1998.2 8.0 all-to-all-start
  (64 other events, 559.7 us)
Sparse Core Ops, SparseCore 0:
  251.3 223.9 all-reduce.42
  575.0 424.0 all-gather.5
  1195.1 108.9 reduce-scatter.16
  1312.1 115.8 all-gather.3
  1758.3 108.9 reduce-scatter.18
  1886.7 29.8 reduce-scatter.28
  1920.2 32.4 reduce-scatter.32
  1955.9 34.9 reduce-scatter.30
  1994.8 42.3 reduce-scatter.26
  2041.0 42.3 reduce-scatter.24
  2087.3 40.1 reduce-scatter.22
  2131.4 47.9 reduce-scatter.20
